TPU v7x, 32 devices: a whole 2x2x4 slice. The times are simulated.
32 devices in a mesh: cell: 16 (over z, y, x), gene: 2 (over core).
Axes of the slice: x: 2, y: 2, z: 4, core: 2. Of those that a mesh axis runs over, the one named last changes fastest.
Arguments:
- tiles: bfloat16 [2, 1024, 128, 128], P('gene', 'cell'), may hold values from -8 to 8
- tile_row: int32 [2, 1024], P('gene', 'cell'), may hold values from 0 to 7, as said below
- tile_col: int32 [2, 1024], P('gene', 'cell'), may hold values from 0 to 15
- tile_count: int32 [2, 16], P('gene', 'cell'), may hold values from 1 to 64, as said below
- start_basis: bfloat16 [64, 4096], P(None, 'gene'), may hold values from -0.09375 to 0.09375
Outputs:
- basis: bfloat16 [64, 16384], P(None, 'cell')
- loadings: float32 [64, 4096], P(None, ('gene', 'cell'))
Inputs may be any that keep to these rules, and one draw needn't show every extreme that they name: `tile_row`: tile row of each slot, within 0 to 7; the slots of one device name distinct (row, column) pairs. `tile_count`: slots in use; for each index of gene some device uses all 64.
All inputs are finite; a program needn't handle non-finite values.
Results may differ from a plain program's by a relative error of at most 0.018.
Values may be sent and summed in bfloat16 or wider, within the bound.
A program may use at most 64 MiB of HBM per device.

v0:
```python
import jax
import jax.numpy as jnp
from jax import lax
from jax.sharding import PartitionSpec as P

ROW_BLOCKS = 8


def solve_lower(lower, right):
    return lax.linalg.triangular_solve(lower, right, left_side=True, lower=True)


def gram_of(scores):
    return jnp.dot(
        scores, scores.T, precision=lax.Precision.HIGHEST, preferred_element_type=jnp.float32
    )


def orthonormal(scores, first_total):
    first = first_total(gram_of(scores))
    lower_one = jnp.linalg.cholesky(first)
    return solve_lower(lower_one, scores)


def local(tiles, tile_row, tile_col, tile_count, start_basis):
    blocks_local = tiles[0]
    slot_count = blocks_local.shape[0]
    tile_size = blocks_local.shape[-1]
    width = start_basis.shape[0]
    gene_dev = start_basis.shape[1]
    gene_blocks = gene_dev // tile_size
    row_blocks = ROW_BLOCKS
    cell_dev = row_blocks * tile_size
    row_index = tile_row[0]
    col_index = tile_col[0]
    live = jnp.arange(slot_count) < tile_count[0, 0]
    row_target = jnp.where(live, row_index, row_blocks)
    col_target = jnp.where(live, col_index, gene_blocks)

    def first_total(gram):
        return lax.psum(gram, ("cell", "gene"))

    def merge_halves(partial_scores):
        return lax.psum_scatter(partial_scores, "gene", scatter_dimension=1, tiled=True)

    def scores_of(basis):
        picked = jnp.take(basis.reshape(width, gene_blocks, tile_size), col_index, axis=1)
        products = jnp.einsum(
            "ksg,srg->skr", picked, blocks_local, preferred_element_type=jnp.float32
        )
        summed = jax.ops.segment_sum(products, row_target, num_segments=row_blocks + 1)[:row_blocks]
        return merge_halves(jnp.transpose(summed, (1, 0, 2)).reshape(width, cell_dev))

    def loadings_of(ortho_half):
        picked = jnp.take(ortho_half.reshape(width, row_blocks, tile_size), row_index, axis=1)
        products = jnp.einsum(
            "ksr,srg->skg", picked, blocks_local, preferred_element_type=jnp.float32
        )
        summed = jax.ops.segment_sum(products, col_target, num_segments=gene_blocks + 1)[
            :gene_blocks
        ]
        return jnp.transpose(summed, (1, 0, 2)).reshape(width, gene_dev)

    ortho = orthonormal(scores_of(start_basis), first_total)
    ortho_half = ortho.astype(jnp.bfloat16)
    ortho_rows = lax.all_gather(ortho_half, "gene", axis=1, tiled=True)
    partial_value = loadings_of(ortho_rows)
    next_basis = lax.psum(partial_value, "cell").astype(jnp.bfloat16)
    ortho_two = orthonormal(scores_of(next_basis), first_total)
    scale = jnp.sqrt(jnp.float32(lax.axis_size("cell") * cell_dev))
    ortho_two_half = ortho_two.astype(jnp.bfloat16)
    basis_piece = (ortho_two * scale).astype(jnp.bfloat16)
    final_rows, basis = (
        lax.all_gather(ortho_two_half, "gene", axis=1, tiled=True),
        lax.all_gather(basis_piece, "gene", axis=1, tiled=True),
    )
    loadings = lax.psum_scatter(loadings_of(final_rows), "cell", scatter_dimension=1, tiled=True)
    return (basis, loadings)


def solution(mesh):
    return jax.shard_map(
        local,
        mesh=mesh,
        in_specs=(
            P("gene", "cell", None, None),
            P("gene", "cell"),
            P("gene", "cell"),
            P("gene", "cell"),
            P(None, "gene"),
        ),
        out_specs=(P(None, "cell"), P(None, ("gene", "cell"))),
        check_vma=False,
    )
```

profile of v0, /device:TPU:0, one launch (start us, length us, event | category | flops | bytes accessed | tf_op | source)
XLA Modules:
  0.0 349.9 jit_solution(15291023441210544630)
XLA Ops:
  7.2 0.0 reduce-scatter.4.cloned.1.call-start
  7.2 0.8 compare_select_fusion
  8.0 0.7 compare_and_fusion
  8.7 1.0 copy_bitcast_fusion.5
  10.4 0.7 gather_fusion
  11.2 2.9 fusion.6
  14.1 7.1 %scatter_fusion = f32[9,64,128]{2,1,0:T(8,128)S(1)} fusion(f32[9,64,128]{2,1,0:T(8,128)S(1)} %broadcast.69.clone, s32[64]{0:T(128)S(1)} %get-tuple-element.8, f32[64,64,128]{2,1,0:T(8,128)} %fusion.6), kind=kCustom, calls=%fused_computation.4 | custom fusion | flops 524288 | bytes 6291712 | tf_op jit(solution)/shard_map/scatter-add | solution.py:51
  21.2 0.7 copy_bitcast_fusion.3
  21.9 0.0 reduce-scatter.6.cloned.1.call-start
  22.0 10.5 %reduce-scatter.4.cloned.1.call-done = f32[64,512]{1,0:T(8,128)} async-done(((f32[64,1024]{1,0:T(8,128)}), f32[64,512]{1,0:T(8,128)}) %reduce-scatter.4.cloned.1.call-update) | async-done | bytes 131088 | tf_op jit(solution)/shard_map/reduce_scatter | solution.py:44
  32.5 1.2 fusion.40
  33.8 40.6 %psum.21 = f32[64,64]{0,1:T(8,128)S(1)} all-reduce(f32[64,64]{0,1:T(8,128)S(1)} %fusion.40), channel_id=1, replica_groups=mesh['cell'=16,'gene'=2] {'cell','gene'}, use_global_device_ids=true, to_apply=%region_2.4 | all-reduce | flops 4096 | bytes 32768 | tf_op jit(solution)/shard_map/psum | solution.py:41
  74.4 0.1 copy.20
  74.5 5.8 %cholesky.44 = f32[64,64]{1,0:T(8,128)S(1)} custom-call(f32[64,64]{1,0:T(8,128)S(1)} %fusion.30), custom_call_target="Cholesky" | custom-call | tf_op jit(solution)/shard_map/jit(cholesky)/cholesky | solution.py:21
  80.3 0.6 compare_reduce_fusion.1
  81.0 0.7 fusion.24
  81.6 4.9 %custom-call.6 = f32[1,64,64]{1,2,0:T(8,128)S(1)} custom-call(f32[1,64,64]{2,1,0:T(8,128)S(1)} %fusion.24), custom_call_target="InvertDiagBlocksLowerTriangular" | custom-call | tf_op jit(solution)/shard_map/triangular_solve/custom-call.0 | solution.py:10
  86.5 1.2 convolution_convert_fusion
  87.8 1.9 all_gather.9
  89.7 0.7 gather_fusion.1
  90.5 2.1 fusion.4
  92.6 7.1 %scatter_fusion.1 = f32[17,64,128]{2,1,0:T(8,128)S(1)} fusion(f32[17,64,128]{2,1,0:T(8,128)S(1)} %broadcast.70.clone, s32[64]{0:T(128)S(1)} %get-tuple-element.9, f32[64,64,128]{2,1,0:T(8,128)} %fusion.4), kind=kCustom, calls=%fused_computation.5 | custom fusion | flops 524288 | bytes 6291712 | tf_op jit(solution)/shard_map/scatter-add | solution.py:59
  99.7 81.7 %all-reduce.1 = bf16[64,2048]{1,0:T(8,128)(2,1)S(1)} all-reduce(f32[64,2048]{1,0:T(8,128)S(1)} %copy_bitcast_fusion.1), channel_id=1, replica_groups=mesh['cell'=16,'gene'=2] {'cell'}, use_global_device_ids=true, to_apply=%region_6.11 | all-reduce | flops 131072 | bytes 786432 | tf_op jit(solution)/shard_map/psum | solution.py:68
  181.4 0.1 copy_bitcast_fusion.4
  181.4 0.8 gather_fusion.2
  182.2 2.9 fusion.2
  185.1 7.1 %scatter_fusion.2 = f32[9,64,128]{2,1,0:T(8,128)S(1)} fusion(f32[9,64,128]{2,1,0:T(8,128)S(1)} %broadcast.69, s32[64]{0:T(128)S(1)} %get-tuple-element.8, f32[64,64,128]{2,1,0:T(8,128)} %fusion.2), kind=kCustom, calls=%fused_computation.6 | custom fusion | flops 524288 | bytes 6291712 | tf_op jit(solution)/shard_map/scatter-add | solution.py:51
  192.2 0.7 copy_bitcast_fusion.2
  192.9 0.0 reduce-scatter.6.cloned.1.call-update
  192.9 0.0 reduce-scatter.8.cloned.1.call-start
  193.0 4.2 %reduce-scatter.6.cloned.1.call-done = f32[64,512]{1,0:T(8,128)} async-done(((f32[64,1024]{1,0:T(8,128)}), f32[64,512]{1,0:T(8,128)}) %reduce-scatter.6.cloned.1.call-update) | async-done | bytes 131088 | tf_op jit(solution)/shard_map/reduce_scatter | solution.py:44
  197.2 1.2 fusion.41
  198.4 40.8 %psum.23 = f32[64,64]{0,1:T(8,128)S(1)} all-reduce(f32[64,64]{0,1:T(8,128)S(1)} %fusion.41), channel_id=1, replica_groups=mesh['cell'=16,'gene'=2] {'cell','gene'}, use_global_device_ids=true, to_apply=%region_9.14 | all-reduce | flops 4096 | bytes 32768 | tf_op jit(solution)/shard_map/psum | solution.py:41
  239.2 0.1 copy.26
  239.3 5.8 %cholesky.55 = f32[64,64]{1,0:T(8,128)S(1)} custom-call(f32[64,64]{1,0:T(8,128)S(1)} %fusion.28), custom_call_target="Cholesky" | custom-call | tf_op jit(solution)/shard_map/jit(cholesky)/cholesky | solution.py:21
  245.2 0.6 compare_reduce_fusion
  245.8 0.7 fusion.25
  246.5 4.9 %custom-call.7 = f32[1,64,64]{1,2,0:T(8,128)S(1)} custom-call(f32[1,64,64]{2,1,0:T(8,128)S(1)} %fusion.25), custom_call_target="InvertDiagBlocksLowerTriangular" | custom-call | tf_op jit(solution)/shard_map/triangular_solve/custom-call.0 | solution.py:10
  251.4 1.2 fusion.39
  252.6 1.9 all_gather.11
  254.5 0.7 gather_fusion.3
  255.3 2.1 fusion
  257.4 7.1 %scatter_fusion.3 = f32[17,64,128]{2,1,0:T(8,128)S(1)} fusion(f32[17,64,128]{2,1,0:T(8,128)S(1)} %broadcast.70, s32[64]{0:T(128)S(1)} %get-tuple-element.9, f32[64,64,128]{2,1,0:T(8,128)} %fusion), kind=kCustom, calls=%fused_computation.7 | custom fusion | flops 524288 | bytes 6291712 | tf_op jit(solution)/shard_map/scatter-add | solution.py:59
  264.5 0.8 copy_bitcast_fusion
  265.3 0.0 reduce-scatter.8.cloned.1.call-update
  265.3 1.9 all_gather.10
  267.2 75.5 %reduce-scatter.8.cloned.1.call-done = f32[64,128]{1,0:T(8,128)} async-done(((f32[64,2048]{1,0:T(8,128)}), f32[64,128]{1,0:T(8,128)}) %reduce-scatter.8.cloned.1.call-update) | async-done | bytes 32784 | tf_op jit(solution)/shard_map/reduce_scatter | solution.py:77
  342.8 0.7 copy.55
  (23 shorter events, 0.4 us)
Async XLA Ops:
  7.2 4.0 %copy-start = (bf16[1,64,128,128]{3,2,1,0:T(8,128)(2,1)S(1)}, bf16[1,64,128,128]{3,2,1,0:T(8,128)(2,1)}, u32[]{:S(2)}) copy-start(bf16[1,64,128,128]{3,2,1,0:T(8,128)(2,1)} %param.12) | copy-start | bytes 6291460
  7.2 4.0 %copy-start.1 = (s32[1,64]{1,0:T(1,128)S(1)}, s32[1,64]{1,0:T(1,128)}, u32[]{:S(2)}) copy-start(s32[1,64]{1,0:T(1,128)} %param.14) | copy-start | bytes 772
  7.2 4.0 %copy-start.2 = (s32[1,64]{1,0:T(1,128)S(1)}, s32[1,64]{1,0:T(1,128)}, u32[]{:S(2)}) copy-start(s32[1,64]{1,0:T(1,128)} %param.13) | copy-start | bytes 772
  7.2 25.3 %reduce-scatter.4.cloned.1.call-start = ((), (), s32[]{:S(2)}) async-start(), calls=%async_computation.3 | async-start | bytes 393216 | tf_op jit(solution)/shard_map/reduce_scatter | solution.py:44
  21.9 175.2 %reduce-scatter.6.cloned.1.call-start = ((), (), s32[]{:S(2)}) async-start(), calls=%async_computation.4 | async-start | bytes 393216 | tf_op jit(solution)/shard_map/reduce_scatter | solution.py:44
  192.9 149.8 %reduce-scatter.8.cloned.1.call-start = ((), (), s32[]{:S(2)}) async-start(), calls=%async_computation.5 | async-start | bytes 557056 | tf_op jit(solution)/shard_map/reduce_scatter | solution.py:77
Sparse Core Ops, SparseCore 0:
  22.0 10.4 reduce-scatter.3
  193.1 4.0 reduce-scatter.5
  265.5 77.2 reduce-scatter.7
where the time goes:
time: 351 us; the launch traced here: 350 us
  blocking collectives  169 us (48%)
  waiting for transfers between devices  90.3 us (26%)
  other arithmetic  53.9 us (15%)
  matrix products  14.9 us (4%)
  between operations  14.7 us (4%)
  local copies, waits for them, and re-layouts  7.35 us (2%)
    psum x1, blocking collectives, local(): next_basis = lax.psum(partial_value, 'cell').astype(jnp.bfloat16)  81.7 us
    psum x2, blocking collectives, first_total(): return lax.psum(gram, ('cell', 'gene'))  81.4 us
    reduce_scatter x1, waiting for transfers between devices, local(): lax.psum_scatter(loadings_of(final_rows), 'cell', scatter_dimension=1, ti...  75.5 us
    reduce_scatter x2, waiting for transfers between devices, merge_halves(): lax.psum_scatter(partial_scores, 'gene', scatter_dimension=1, tiled=True)  14.7 us
    scatter-add x2, other arithmetic, scores_of(): jax.ops.segment_sum(products, row_target, num_segments=row_blocks + 1)  14.1 us
    scatter-add x2, other arithmetic, loadings_of(): jax.ops.segment_sum(products, col_target, num_segments=gene_blocks + 1)  14.1 us
    another operation x6, other arithmetic, orthonormal(): lower_one = jnp.linalg.cholesky(first)  13 us
    another operation x4, other arithmetic, solve_lower(): return lax.linalg.triangular_solve(lower, right, left_side=True, lower=True)  11.1 us
  transfers between devices with their start and end apart: 3, of which 3 were waited for; matrix products, arithmetic and copies ran while one was open for 0% of the time, Pallas kernels for 0%

commit v1 on v0

v1 whole, which is shorter than its diff:
```python
import functools

import jax
import jax.numpy as jnp
from jax import lax
from jax.experimental import pallas as pl
from jax.experimental.pallas import tpu as pltpu
from jax.sharding import PartitionSpec as P

ROW_BLOCKS = 8
PANEL = 4
MESH = pl.DeviceIdType.MESH
HIGH = lax.Precision.HIGHEST


def split_three(value):
    high = value.astype(jnp.bfloat16)
    rest = value - high.astype(jnp.float32)
    middle = rest.astype(jnp.bfloat16)
    low = (rest - middle.astype(jnp.float32)).astype(jnp.bfloat16)
    return high, middle, low


def inverse_factor(gram):
    width = gram.shape[0]
    shape = (width, 2 * width)
    row = lax.broadcasted_iota(jnp.int32, shape, 0)
    lane = lax.broadcasted_iota(jnp.int32, shape, 1)
    both = jnp.concatenate([jnp.zeros_like(gram), gram], axis=1)
    both = jnp.where(row == lane, 1.0, both)
    pivots = jnp.ones(shape, jnp.float32)
    done = []
    start = 0
    for first in range(0, width, PANEL):
        base = first // 8 * 8
        if base > start:
            done.append((both[: base - start], pivots[: base - start]))
            both = both[base - start :]
            pivots = pivots[base - start :]
            row = row[base - start :]
            start = base
        columns = [
            jnp.broadcast_to(both[:, width + j : width + j + 1], both.shape)
            for j in range(first, first + PANEL)
        ]
        for k in range(PANEL):
            j = first + k
            at = j - start
            pivot = columns[k][at : at + 1]
            factor = jnp.where(row > j, columns[k] * (1.0 / pivot), 0.0)
            pivots = jnp.where(row == j, pivot, pivots)
            both = both - factor * both[at : at + 1]
            for m in range(k + 1, PANEL):
                columns[m] = columns[m] - factor * columns[m][at : at + 1]
    done.append((both, pivots))
    both = jnp.concatenate([piece for piece, _ in done], axis=0)
    pivots = jnp.concatenate([piece for _, piece in done], axis=0)
    return (both * lax.rsqrt(pivots))[:, :width]


def kernel(
    cells, genes, parts,
    table, tiles, start, basis_out, load_out,
    held, dense, mine, theirs, stacked, grams, sums_out, sums_in, middle,
    tile_sem, pair_send, pair_recv, gram_send, gram_recv,
    sum_send, sum_recv, mid_send, mid_recv,
):
    cell = lax.axis_index("cell")
    gene = lax.axis_index("gene")
    slots, side, _ = tiles.shape
    width = start.shape[0]
    cell_dev, gene_dev = dense.shape
    gene_blocks = gene_dev // side
    chunk = gene_dev // cells
    piece = cell_dev // parts
    half = width // 2
    other = lax.rem(gene + 1, genes)

    fetch = pltpu.make_async_copy(tiles, held.at[pl.ds(0, slots)], tile_sem)
    fetch.start()

    barrier = pltpu.get_barrier_semaphore()

    def greet(k, _):
        pl.semaphore_signal(
            barrier, inc=1, device_id={"cell": lax.rem(cell + k, cells)}, device_id_type=MESH
        )
        return 0

    pl.semaphore_signal(barrier, inc=1, device_id={"gene": other}, device_id_type=MESH)
    lax.fori_loop(1, cells, greet, 0)
    held[slots] = jnp.zeros((side, side), held.dtype)
    fetch.wait()

    def place(i, _):
        row = i // gene_blocks
        col = lax.rem(i, gene_blocks)
        dense[
            pl.ds(pl.multiple_of(row * side, side), side),
            pl.ds(pl.multiple_of(col * side, side), side),
        ] = held[table[i]]
        return 0

    lax.fori_loop(0, (cell_dev // side) * gene_blocks, place, 0)
    pl.semaphore_wait(barrier, cells)

    def pair_copy(it, r):
        return pltpu.make_async_remote_copy(
            src_ref=mine.at[it, r], dst_ref=theirs.at[it, r],
            send_sem=pair_send.at[it, r], recv_sem=pair_recv.at[it, r],
            device_id={"gene": other}, device_id_type=MESH,
        )

    def gram_copy(it, source, k):
        return pltpu.make_async_remote_copy(
            src_ref=grams.at[it, source], dst_ref=grams.at[it, source],
            send_sem=gram_send.at[it, k], recv_sem=gram_recv.at[it, source],
            device_id={"cell": lax.rem(cell + k, cells)}, device_id_type=MESH,
        )

    def sum_copy(it, source, k):
        target = lax.rem(cell + k, cells)
        return pltpu.make_async_remote_copy(
            src_ref=sums_out.at[it, target], dst_ref=sums_in.at[it, source],
            send_sem=sum_send.at[it, k], recv_sem=sum_recv.at[it, source],
            device_id={"cell": target}, device_id_type=MESH,
        )

    def mid_copy(source, k):
        return pltpu.make_async_remote_copy(
            src_ref=middle.at[source], dst_ref=middle.at[source],
            send_sem=mid_send.at[k], recv_sem=mid_recv.at[source],
            device_id={"cell": lax.rem(cell + k, cells)}, device_id_type=MESH,
        )

    def each(act):
        def body(k, _):
            act(lax.rem(cell + cells - k, cells), k)
            return 0

        lax.fori_loop(1, cells, body, 0)

    for it in range(2):
        if it == 0:
            basis = start[...]
        else:
            basis = jnp.concatenate([middle[c] for c in range(cells)], axis=1)

        for r in range(parts):
            mine[it, r] = lax.dot_general(
                basis, dense[r * piece : (r + 1) * piece, :], (((1,), (1,)), ((), ())),
                preferred_element_type=jnp.float32,
            )
            pair_copy(it, r).start()
        for r in range(parts):
            pair_copy(it, r).wait_recv()
            where = slice(r * piece, (r + 1) * piece)
            high, mid, low = split_three(mine[it, r] + theirs[it, r])
            stacked[0:width, where] = high
            stacked[width : 2 * width, where] = mid
            stacked[2 * width : 3 * width, where] = low

        whole = stacked[...]
        cross = lax.dot_general(
            whole, whole, (((1,), (1,)), ((), ())), preferred_element_type=jnp.float32
        )
        cross = cross[:width] + cross[width : 2 * width] + cross[2 * width :]
        gram = cross[:, :width] + cross[:, width : 2 * width] + cross[:, 2 * width :]
        grams[it, cell] = jnp.concatenate([gram[:half], gram[half:]], axis=1)
        each(lambda _, k: gram_copy(it, cell, k).start())

        def product(columns):
            pair = jnp.dot(
                stacked[0 : 2 * width, :], columns, preferred_element_type=jnp.float32
            )
            return pair[:width] + pair[width:]

        if chunk % 128 == 0:

            def send(k, _):
                target = lax.rem(cell + k, cells)
                sums_out[it, target] = product(
                    dense[:, pl.ds(pl.multiple_of(target * chunk, chunk), chunk)]
                )
                sum_copy(it, cell, k).start()
                return 0

            lax.fori_loop(1, cells, send, 0)
            sums_in[it, cell] = product(
                dense[:, pl.ds(pl.multiple_of(cell * chunk, chunk), chunk)]
            )
        else:
            for b in range(gene_blocks):
                wide = product(dense[:, b * side : (b + 1) * side])
                for c in range(side // chunk):
                    sums_out[it, b * (side // chunk) + c] = wide[:, c * chunk : (c + 1) * chunk]
            each(lambda _, k: sum_copy(it, cell, k).start())
            sums_in[it, cell] = sums_out[it, cell]

        each(lambda source, k: gram_copy(it, source, k).wait_recv())
        total = grams[it, 0]
        for c in range(1, cells):
            total = total + grams[it, c]
        total = jnp.concatenate([total[:, :width], total[:, width:]], axis=0)
        inverse = inverse_factor(total)

        if it == 1:
            scale = jnp.sqrt(jnp.float32(cells * cell_dev))
            for r in range(parts):
                basis_out[:, r * piece : (r + 1) * piece] = (
                    jnp.dot(
                        inverse, mine[it, r] + theirs[it, r], precision=HIGH,
                        preferred_element_type=jnp.float32,
                    ) * scale
                ).astype(basis_out.dtype)

        each(lambda source, k: sum_copy(it, source, k).wait_recv())
        summed = sums_in[it, 0]
        for c in range(1, cells):
            summed = summed + sums_in[it, c]
        result = jnp.dot(inverse, summed, precision=HIGH, preferred_element_type=jnp.float32)
        if it == 0:
            middle[cell] = result.astype(middle.dtype)
            each(lambda _, k: mid_copy(cell, k).start())
            each(lambda source, k: mid_copy(source, k).wait_recv())
        else:
            load_out[...] = result

    for it in range(2):
        for r in range(parts):
            pair_copy(it, r).wait_send()
        each(lambda _, k: gram_copy(it, cell, k).wait_send())
        each(lambda _, k: sum_copy(it, cell, k).wait_send())
    each(lambda _, k: mid_copy(cell, k).wait_send())


def local(cells, genes, tiles, tile_row, tile_col, tile_count, start_basis):
    slots, side = tiles.shape[1], tiles.shape[-1]
    width, gene_dev = start_basis.shape
    gene_blocks = gene_dev // side
    cell_dev = ROW_BLOCKS * side
    chunk = gene_dev // cells
    parts = 4
    places = ROW_BLOCKS * gene_blocks
    live = jnp.arange(slots) < tile_count[0, 0]
    spot = jnp.where(live, tile_row[0] * gene_blocks + tile_col[0], places)
    table = jnp.min(
        jnp.where(spot[None, :] == jnp.arange(places)[:, None], jnp.arange(slots)[None, :], slots),
        axis=1,
    ).astype(jnp.int32)
    dma = pltpu.SemaphoreType.DMA
    return pl.pallas_call(
        functools.partial(kernel, cells, genes, parts),
        out_shape=(
            jax.ShapeDtypeStruct((width, cell_dev), jnp.bfloat16),
            jax.ShapeDtypeStruct((width, chunk), jnp.float32),
        ),
        in_specs=[
            pl.BlockSpec(memory_space=pltpu.SMEM),
            pl.BlockSpec(memory_space=pl.ANY),
            pl.BlockSpec(memory_space=pltpu.VMEM),
        ],
        out_specs=(
            pl.BlockSpec(memory_space=pltpu.VMEM),
            pl.BlockSpec(memory_space=pltpu.VMEM),
        ),
        scratch_shapes=[
            pltpu.VMEM((slots + 1, side, side), jnp.bfloat16),
            pltpu.VMEM((cell_dev, gene_dev), jnp.bfloat16),
            pltpu.VMEM((2, parts, width, cell_dev // parts), jnp.float32),
            pltpu.VMEM((2, parts, width, cell_dev // parts), jnp.float32),
            pltpu.VMEM((3 * width, cell_dev), jnp.bfloat16),
            pltpu.VMEM((2, cells, width // 2, 2 * width), jnp.float32),
            pltpu.VMEM((2, cells, width, chunk), jnp.float32),
            pltpu.VMEM((2, cells, width, chunk), jnp.float32),
            pltpu.VMEM((cells, width, chunk), jnp.bfloat16),
            dma,
            dma((2, parts)), dma((2, parts)),
            dma((2, cells)), dma((2, cells)),
            dma((2, cells)), dma((2, cells)),
            dma((cells,)), dma((cells,)),
        ],
        compiler_params=pltpu.CompilerParams(
            collective_id=0, has_side_effects=True, vmem_limit_bytes=60 * 1024 * 1024
        ),
    )(table, tiles[0], start_basis)


def solution(mesh):
    return jax.shard_map(
        functools.partial(local, mesh.shape["cell"], mesh.shape["gene"]),
        mesh=mesh,
        in_specs=(
            P("gene", "cell", None, None),
            P("gene", "cell"),
            P("gene", "cell"),
            P("gene", "cell"),
            P(None, "gene"),
        ),
        out_specs=(P(None, "cell"), P(None, ("gene", "cell"))),
        check_vma=False,
    )
```

time: 351 us -> 67.6 us (0.19)
  the two profiles are of different devices: /device:TPU:0 before, /device:TPU:15 now
where the time goes in v1:
time: 67.6 us; the launch traced here: 67.3 us
  Pallas kernels  61.8 us (91%)
  local copies, waits for them, and re-layouts  2.94 us (4%)
  between operations  1.29 us (2%)
  other arithmetic  1.28 us (2%)
    pallas_call x1, Pallas kernels, local(): pl.pallas_call(functools.partial(kernel, cells, genes, parts), out_shape=...  61.8 us
    unnamed x2, local copies, waits for them, and re-layouts  2.94 us

profile of v1, /device:TPU:15, one launch (start us, length us, event | category | flops | bytes accessed | tf_op | source)
XLA Modules:
  0.0 67.3 jit_solution(5279718843828514475)
XLA Ops:
  1.3 0.7 %fusion = s32[64]{0:T(128)S(1)} fusion(s32[1,64]{1,0:T(1,128)} %param.7, s32[1,64]{1,0:T(1,128)} %param.6, s32[]{:T(128)} %bitcast.4), kind=kLoop, calls=%fused_computation.3 | loop fusion | flops 256 | bytes 772 | tf_op jit(solution)/shard_map/eq | solution.py:248
  2.0 0.6 select_reduce_fusion.table
  2.6 61.8 %shard_map.68 = (bf16[64,1024]{1,0:T(8,128)(2,1)}, f32[64,128]{1,0:T(8,128)}) custom-call(s32[128]{0:T(128)} %select_reduce_fusion.table, bf16[64,128,128]{2,1,0:T(8,128)(2,1)} %bitcast.5, bf16[64,2048]{1,0:T(8,128)(2,1)} %start.1), custom_call_target="tpu_custom_call" | custom-call | tf_op jit(solution)/shard_map/pallas_call | solution.py:252
  64.4 1.6 %copy.10 = bf16[64,1024]{1,0:T(8,128)(2,1)} copy(bf16[64,1024]{1,0:T(8,128)(2,1)} %get-tuple-element.4) | data formatting | bytes 262144
  65.9 1.4 %copy.11 = f32[64,128]{1,0:T(8,128)} copy(f32[64,128]{1,0:T(8,128)} %get-tuple-element.5) | data formatting | bytes 65536

commit v2 on v1

--- a/solution.py
+++ b/solution.py
@@ -59,11 +59,11 @@
 
 
 def kernel(
-    cells, genes, parts,
+    cells, inner, genes, parts,
     table, tiles, start, basis_out, load_out,
-    held, dense, mine, theirs, stacked, grams, sums_out, sums_in, middle,
-    tile_sem, pair_send, pair_recv, gram_send, gram_recv,
-    sum_send, sum_recv, mid_send, mid_recv,
+    held, dense, mine, theirs, stacked, grams, planes, sums_out, sums_mid, sums_own, sums_in, middle,
+    tile_sem, pair_send, pair_recv, gram_send, gram_recv, plane_send, plane_recv,
+    near_send, near_recv, far_send, far_recv, mid_send, mid_recv,
 ):
     cell = lax.axis_index("cell")
     gene = lax.axis_index("gene")
@@ -74,6 +74,9 @@
     chunk = gene_dev // cells
     piece = cell_dev // parts
     half = width // 2
+    outer = cells // inner
+    here = cell // inner
+    spot = lax.rem(cell, inner)
     other = lax.rem(gene + 1, genes)
 
     fetch = pltpu.make_async_copy(tiles, held.at[pl.ds(0, slots)], tile_sem)
@@ -111,19 +114,39 @@
             device_id={"gene": other}, device_id_type=MESH,
         )
 
+    def near(k):
+        return here * inner + lax.rem(spot + k, inner)
+
+    def far(k):
+        return lax.rem(here + k, outer) * inner + spot
+
     def gram_copy(it, source, k):
         return pltpu.make_async_remote_copy(
             src_ref=grams.at[it, source], dst_ref=grams.at[it, source],
             send_sem=gram_send.at[it, k], recv_sem=gram_recv.at[it, source],
-            device_id={"cell": lax.rem(cell + k, cells)}, device_id_type=MESH,
-        )
-
-    def sum_copy(it, source, k):
-        target = lax.rem(cell + k, cells)
-        return pltpu.make_async_remote_copy(
-            src_ref=sums_out.at[it, target], dst_ref=sums_in.at[it, source],
-            send_sem=sum_send.at[it, k], recv_sem=sum_recv.at[it, source],
-            device_id={"cell": target}, device_id_type=MESH,
+            device_id={"cell": near(k)}, device_id_type=MESH,
+        )
+
+    def plane_copy(it, source, k):
+        return pltpu.make_async_remote_copy(
+            src_ref=planes.at[it, source], dst_ref=planes.at[it, source],
+            send_sem=plane_send.at[it, k], recv_sem=plane_recv.at[it, source],
+            device_id={"cell": far(k)}, device_id_type=MESH,
+        )
+
+    def near_copy(it, group, source, k):
+        return pltpu.make_async_remote_copy(
+            src_ref=sums_out.at[it, group, lax.rem(spot + k, inner)],
+            dst_ref=sums_mid.at[it, group, source],
+            send_sem=near_send.at[it, group, k], recv_sem=near_recv.at[it, group, source],
+            device_id={"cell": near(k)}, device_id_type=MESH,
+        )
+
+    def far_copy(it, source, k):
+        return pltpu.make_async_remote_copy(
+            src_ref=sums_own.at[it, lax.rem(here + k, outer)], dst_ref=sums_in.at[it, source],
+            send_sem=far_send.at[it, k], recv_sem=far_recv.at[it, source],
+            device_id={"cell": far(k)}, device_id_type=MESH,
         )
 
     def mid_copy(source, k):
@@ -139,6 +162,20 @@
             return 0
 
         lax.fori_loop(1, cells, body, 0)
+
+    def each_near(act):
+        for k in range(1, inner):
+            act(lax.rem(spot + inner - k, inner), k)
+
+    def each_far(act):
+        for k in range(1, outer):
+            act(lax.rem(here + outer - k, outer), k)
+
+    def added(ref, count):
+        total = ref[0]
+        for c in range(1, count):
+            total = total + ref[c]
+        return total
 
     for it in range(2):
         if it == 0:
@@ -166,8 +203,8 @@
         )
         cross = cross[:width] + cross[width : 2 * width] + cross[2 * width :]
         gram = cross[:, :width] + cross[:, width : 2 * width] + cross[:, 2 * width :]
-        grams[it, cell] = jnp.concatenate([gram[:half], gram[half:]], axis=1)
-        each(lambda _, k: gram_copy(it, cell, k).start())
+        grams[it, spot] = jnp.concatenate([gram[:half], gram[half:]], axis=1)
+        each_near(lambda _, k: gram_copy(it, spot, k).start())
 
         def product(columns):
             pair = jnp.dot(
@@ -175,32 +212,45 @@
             )
             return pair[:width] + pair[width:]
 
-        if chunk % 128 == 0:
-
-            def send(k, _):
-                target = lax.rem(cell + k, cells)
-                sums_out[it, target] = product(
-                    dense[:, pl.ds(pl.multiple_of(target * chunk, chunk), chunk)]
-                )
-                sum_copy(it, cell, k).start()
-                return 0
-
-            lax.fori_loop(1, cells, send, 0)
-            sums_in[it, cell] = product(
-                dense[:, pl.ds(pl.multiple_of(cell * chunk, chunk), chunk)]
-            )
-        else:
+        span = inner * chunk
+
+        def multiply(k):
+            group = lax.rem(here + k, outer)
+            if span % 128 == 0:
+                wide = product(dense[:, pl.ds(pl.multiple_of(group * span, 128), span)])
+                for c in range(inner):
+                    sums_out[it, group, c] = wide[:, c * chunk : (c + 1) * chunk]
+            each_near(lambda _, k: near_copy(it, group, spot, k).start())
+
+        def forward(k):
+            group = lax.rem(here + k, outer)
+            each_near(lambda source, k: near_copy(it, group, source, k).wait_recv())
+            total = sums_out[it, group, spot]
+            for c in range(1, inner):
+                total = total + sums_mid[it, group, lax.rem(spot + c, inner)]
+            if k == 0:
+                sums_in[it, here] = total
+            else:
+                sums_own[it, group] = total
+                far_copy(it, here, k).start()
+
+        if span % 128 != 0:
             for b in range(gene_blocks):
                 wide = product(dense[:, b * side : (b + 1) * side])
                 for c in range(side // chunk):
-                    sums_out[it, b * (side // chunk) + c] = wide[:, c * chunk : (c + 1) * chunk]
-            each(lambda _, k: sum_copy(it, cell, k).start())
-            sums_in[it, cell] = sums_out[it, cell]
-
-        each(lambda source, k: gram_copy(it, source, k).wait_recv())
-        total = grams[it, 0]
-        for c in range(1, cells):
-            total = total + grams[it, c]
+                    at = b * (side // chunk) + c
+                    sums_out[it, at // inner, at % inner] = wide[:, c * chunk : (c + 1) * chunk]
+        multiply(1)
+        each_near(lambda source, k: gram_copy(it, source, k).wait_recv())
+        planes[it, here] = added(grams.at[it], inner)
+        each_far(lambda _, k: plane_copy(it, here, k).start())
+        for k in range(2, outer):
+            multiply(k)
+        multiply(0)
+        for k in range(1, outer):
+            forward(k)
+        each_far(lambda source, k: plane_copy(it, source, k).wait_recv())
+        total = added(planes.at[it], outer)
         total = jnp.concatenate([total[:, :width], total[:, width:]], axis=0)
         inverse = inverse_factor(total)
 
@@ -214,10 +264,9 @@
                     ) * scale
                 ).astype(basis_out.dtype)
 
-        each(lambda source, k: sum_copy(it, source, k).wait_recv())
-        summed = sums_in[it, 0]
-        for c in range(1, cells):
-            summed = summed + sums_in[it, c]
+        forward(0)
+        each_far(lambda source, k: far_copy(it, source, k).wait_recv())
+        summed = added(sums_in.at[it], outer)
         result = jnp.dot(inverse, summed, precision=HIGH, preferred_element_type=jnp.float32)
         if it == 0:
             middle[cell] = result.astype(middle.dtype)
@@ -229,8 +278,11 @@
     for it in range(2):
         for r in range(parts):
             pair_copy(it, r).wait_send()
-        each(lambda _, k: gram_copy(it, cell, k).wait_send())
-        each(lambda _, k: sum_copy(it, cell, k).wait_send())
+        each_near(lambda _, k: gram_copy(it, spot, k).wait_send())
+        each_far(lambda _, k: plane_copy(it, here, k).wait_send())
+        for group in range(outer):
+            each_near(lambda _, k: near_copy(it, group, spot, k).wait_send())
+        each_far(lambda _, k: far_copy(it, here, k).wait_send())
     each(lambda _, k: mid_copy(cell, k).wait_send())
 
 
@@ -241,6 +293,10 @@
     cell_dev = ROW_BLOCKS * side
     chunk = gene_dev // cells
     parts = 4
+    inner = 1
+    while inner * inner * 4 <= cells and cells % (inner * 2) == 0:
+        inner = inner * 2
+    outer = cells // inner
     places = ROW_BLOCKS * gene_blocks
     live = jnp.arange(slots) < tile_count[0, 0]
     spot = jnp.where(live, tile_row[0] * gene_blocks + tile_col[0], places)
@@ -250,7 +306,7 @@
     ).astype(jnp.int32)
     dma = pltpu.SemaphoreType.DMA
     return pl.pallas_call(
-        functools.partial(kernel, cells, genes, parts),
+        functools.partial(kernel, cells, inner, genes, parts),
         out_shape=(
             jax.ShapeDtypeStruct((width, cell_dev), jnp.bfloat16),
             jax.ShapeDtypeStruct((width, chunk), jnp.float32),
@@ -270,14 +326,17 @@
             pltpu.VMEM((2, parts, width, cell_dev // parts), jnp.float32),
             pltpu.VMEM((2, parts, width, cell_dev // parts), jnp.float32),
             pltpu.VMEM((3 * width, cell_dev), jnp.bfloat16),
-            pltpu.VMEM((2, cells, width // 2, 2 * width), jnp.float32),
-            pltpu.VMEM((2, cells, width, chunk), jnp.float32),
-            pltpu.VMEM((2, cells, width, chunk), jnp.float32),
+            pltpu.VMEM((2, inner, width // 2, 2 * width), jnp.float32),
+            pltpu.VMEM((2, outer, width // 2, 2 * width), jnp.float32),
+            pltpu.VMEM((2, outer, inner, width, chunk), jnp.float32),
+            pltpu.VMEM((2, outer, inner, width, chunk), jnp.float32),
+            pltpu.VMEM((2, outer, width, chunk), jnp.float32),
+            pltpu.VMEM((2, outer, width, chunk), jnp.float32),
             pltpu.VMEM((cells, width, chunk), jnp.bfloat16),
             dma,
             dma((2, parts)), dma((2, parts)),
-            dma((2, cells)), dma((2, cells)),
-            dma((2, cells)), dma((2, cells)),
+            dma((2, inner)), dma((2, inner)), dma((2, outer)), dma((2, outer)),
+            dma((2, outer, inner)), dma((2, outer, inner)), dma((2, outer)), dma((2, outer)),
             dma((cells,)), dma((cells,)),
         ],
         compiler_params=pltpu.CompilerParams(

time: 67.6 us -> 54.9 us (0.81)
  the two profiles are of different devices: /device:TPU:15 before, /device:TPU:0 now
where the time goes in v2:
time: 54.9 us; the launch traced here: 54.6 us
  Pallas kernels  49.1 us (89%)
  local copies, waits for them, and re-layouts  2.94 us (5%)
  between operations  1.29 us (2%)
  other arithmetic  1.28 us (2%)
    pallas_call x1, Pallas kernels, local(): pl.pallas_call(functools.partial(kernel, cells, inner, genes, parts), out...  49.1 us
    unnamed x2, local copies, waits for them, and re-layouts  2.94 us

profile of v2, /device:TPU:0, one launch (start us, length us, event | category | flops | bytes accessed | tf_op | source)
XLA Modules:
  0.0 54.6 jit_solution(13960056884215345585)
XLA Ops:
  1.3 0.7 %fusion = s32[64]{0:T(128)S(1)} fusion(s32[1,64]{1,0:T(1,128)} %param.7, s32[1,64]{1,0:T(1,128)} %param.6, s32[]{:T(128)} %bitcast.4), kind=kLoop, calls=%fused_computation.3 | loop fusion | flops 256 | bytes 772 | tf_op jit(solution)/shard_map/eq | solution.py:304
  2.0 0.6 %select_reduce_fusion.table = s32[128]{0:T(128)} fusion(s32[64]{0:T(128)S(1)} %fusion), kind=kLoop, calls=%fused_computation | loop fusion | flops 24448 | bytes 768 | tf_op jit(solution)/shard_map/reduce_min | solution.py:303
  2.6 49.1 %shard_map.68 = (bf16[64,1024]{1,0:T(8,128)(2,1)}, f32[64,128]{1,0:T(8,128)}) custom-call(s32[128]{0:T(128)} %select_reduce_fusion.table, bf16[64,128,128]{2,1,0:T(8,128)(2,1)} %bitcast.5, bf16[64,2048]{1,0:T(8,128)(2,1)} %start.1), custom_call_target="tpu_custom_call" | custom-call | tf_op jit(solution)/shard_map/pallas_call | solution.py:308
  51.6 1.6 %copy.10 = bf16[64,1024]{1,0:T(8,128)(2,1)} copy(bf16[64,1024]{1,0:T(8,128)(2,1)} %get-tuple-element.4) | data formatting | bytes 262144
  53.2 1.4 %copy.11 = f32[64,128]{1,0:T(8,128)} copy(f32[64,128]{1,0:T(8,128)} %get-tuple-element.5) | data formatting | bytes 65536

commit v3 on v2

--- a/solution.py
+++ b/solution.py
@@ -61,7 +61,7 @@
 def kernel(
     cells, inner, genes, parts,
     table, tiles, start, basis_out, load_out,
-    held, dense, mine, theirs, stacked, grams, planes, sums_out, sums_mid, sums_own, sums_in, middle,
+    held, dense, mine, theirs, stacked, grams, planes, sums_out, sums_mid, sums_own, sums_in, middle, basis,
     tile_sem, pair_send, pair_recv, gram_send, gram_recv, plane_send, plane_recv,
     near_send, near_recv, far_send, far_recv, mid_send, mid_recv,
 ):
@@ -105,6 +105,7 @@
         return 0
 
     lax.fori_loop(0, (cell_dev // side) * gene_blocks, place, 0)
+    basis[...] = start[...]
     pl.semaphore_wait(barrier, cells)
 
     def pair_copy(it, r):
@@ -177,25 +178,33 @@
             total = total + ref[c]
         return total
 
-    for it in range(2):
-        if it == 0:
-            basis = start[...]
-        else:
-            basis = jnp.concatenate([middle[c] for c in range(cells)], axis=1)
-
-        for r in range(parts):
+    def loop(first, last, act):
+        def body(k, _):
+            act(k)
+            return 0
+
+        lax.fori_loop(first, last, body, 0)
+
+    def part(r):
+        return pl.ds(pl.multiple_of(r * piece, piece), piece)
+
+    def iteration(it):
+        def score(r):
             mine[it, r] = lax.dot_general(
-                basis, dense[r * piece : (r + 1) * piece, :], (((1,), (1,)), ((), ())),
+                basis[...], dense[part(r), :], (((1,), (1,)), ((), ())),
                 preferred_element_type=jnp.float32,
             )
             pair_copy(it, r).start()
-        for r in range(parts):
+
+        def merge(r):
             pair_copy(it, r).wait_recv()
-            where = slice(r * piece, (r + 1) * piece)
             high, mid, low = split_three(mine[it, r] + theirs[it, r])
-            stacked[0:width, where] = high
-            stacked[width : 2 * width, where] = mid
-            stacked[2 * width : 3 * width, where] = low
+            stacked[0:width, part(r)] = high
+            stacked[width : 2 * width, part(r)] = mid
+            stacked[2 * width : 3 * width, part(r)] = low
+
+        loop(0, parts, score)
+        loop(0, parts, merge)
 
         whole = stacked[...]
         cross = lax.dot_general(
@@ -228,7 +237,7 @@
             total = sums_out[it, group, spot]
             for c in range(1, inner):
                 total = total + sums_mid[it, group, lax.rem(spot + c, inner)]
-            if k == 0:
+            if isinstance(k, int):
                 sums_in[it, here] = total
             else:
                 sums_own[it, group] = total
@@ -244,45 +253,53 @@
         each_near(lambda source, k: gram_copy(it, source, k).wait_recv())
         planes[it, here] = added(grams.at[it], inner)
         each_far(lambda _, k: plane_copy(it, here, k).start())
-        for k in range(2, outer):
-            multiply(k)
-        multiply(0)
-        for k in range(1, outer):
-            forward(k)
+        loop(2, outer + 1, multiply)
+        loop(1, outer, forward)
         each_far(lambda source, k: plane_copy(it, source, k).wait_recv())
         total = added(planes.at[it], outer)
         total = jnp.concatenate([total[:, :width], total[:, width:]], axis=0)
         inverse = inverse_factor(total)
 
-        if it == 1:
+        @pl.when(it == 1)
+        def _():
             scale = jnp.sqrt(jnp.float32(cells * cell_dev))
-            for r in range(parts):
-                basis_out[:, r * piece : (r + 1) * piece] = (
+
+            def finish(r):
+                basis_out[:, part(r)] = (
                     jnp.dot(
                         inverse, mine[it, r] + theirs[it, r], precision=HIGH,
                         preferred_element_type=jnp.float32,
                     ) * scale
                 ).astype(basis_out.dtype)
 
+            loop(0, parts, finish)
+
         forward(0)
         each_far(lambda source, k: far_copy(it, source, k).wait_recv())
         summed = added(sums_in.at[it], outer)
         result = jnp.dot(inverse, summed, precision=HIGH, preferred_element_type=jnp.float32)
-        if it == 0:
+
+        @pl.when(it == 0)
+        def _():
             middle[cell] = result.astype(middle.dtype)
             each(lambda _, k: mid_copy(cell, k).start())
             each(lambda source, k: mid_copy(source, k).wait_recv())
-        else:
+            basis[...] = jnp.concatenate([middle[c] for c in range(cells)], axis=1)
+
+        @pl.when(it == 1)
+        def _():
             load_out[...] = result
 
-    for it in range(2):
-        for r in range(parts):
-            pair_copy(it, r).wait_send()
+    loop(0, 2, iteration)
+
+    def drain(it):
+        loop(0, parts, lambda r: pair_copy(it, r).wait_send())
         each_near(lambda _, k: gram_copy(it, spot, k).wait_send())
         each_far(lambda _, k: plane_copy(it, here, k).wait_send())
-        for group in range(outer):
-            each_near(lambda _, k: near_copy(it, group, spot, k).wait_send())
+        loop(0, outer, lambda group: each_near(lambda _, k: near_copy(it, group, spot, k).wait_send()))
         each_far(lambda _, k: far_copy(it, here, k).wait_send())
+
+    loop(0, 2, drain)
     each(lambda _, k: mid_copy(cell, k).wait_send())
 
 
@@ -333,6 +350,7 @@
             pltpu.VMEM((2, outer, width, chunk), jnp.float32),
             pltpu.VMEM((2, outer, width, chunk), jnp.float32),
             pltpu.VMEM((cells, width, chunk), jnp.bfloat16),
+            pltpu.VMEM((width, gene_dev), jnp.bfloat16),
             dma,
             dma((2, parts)), dma((2, parts)),
             dma((2, inner)), dma((2, inner)), dma((2, outer)), dma((2, outer)),

time: 54.9 us -> 53.2 us (0.969)
  Pallas kernels: 49.1 us -> 47.4 us
    pallas_call x1, Pallas kernels: 49.1 us -> 47.4 us  [local(): pl.pallas_call(functools.partial(kernel, cells, inner, genes, parts), out...]
where the time goes in v3:
time: 53.2 us; the launch traced here: 52.9 us
  Pallas kernels  47.4 us (89%)
  local copies, waits for them, and re-layouts  2.94 us (6%)
  between operations  1.29 us (2%)
  other arithmetic  1.28 us (2%)
    pallas_call x1, Pallas kernels, local(): pl.pallas_call(functools.partial(kernel, cells, inner, genes, parts), out...  47.4 us
    unnamed x2, local copies, waits for them, and re-layouts  2.94 us

profile of v3, /device:TPU:0, one launch (start us, length us, event | category | flops | bytes accessed | tf_op | source)
XLA Modules:
  0.0 52.9 jit_solution(13710874688166366887)
XLA Ops:
  1.3 0.7 %fusion = s32[64]{0:T(128)S(1)} fusion(s32[1,64]{1,0:T(1,128)} %param.7, s32[1,64]{1,0:T(1,128)} %param.6, s32[]{:T(128)} %bitcast.4), kind=kLoop, calls=%fused_computation.3 | loop fusion | flops 256 | bytes 772 | tf_op jit(solution)/shard_map/eq | solution.py:321
  2.0 0.6 %select_reduce_fusion.table = s32[128]{0:T(128)} fusion(s32[64]{0:T(128)S(1)} %fusion), kind=kLoop, calls=%fused_computation | loop fusion | flops 24448 | bytes 768 | tf_op jit(solution)/shard_map/reduce_min | solution.py:320
  2.6 47.4 %shard_map.68 = (bf16[64,1024]{1,0:T(8,128)(2,1)}, f32[64,128]{1,0:T(8,128)}) custom-call(s32[128]{0:T(128)} %select_reduce_fusion.table, bf16[64,128,128]{2,1,0:T(8,128)(2,1)} %bitcast.5, bf16[64,2048]{1,0:T(8,128)(2,1)} %start.1), custom_call_target="tpu_custom_call" | custom-call | tf_op jit(solution)/shard_map/pallas_call | solution.py:325
  50.0 1.6 %copy.10 = bf16[64,1024]{1,0:T(8,128)(2,1)} copy(bf16[64,1024]{1,0:T(8,128)(2,1)} %get-tuple-element.4) | data formatting | bytes 262144
  51.5 1.4 %copy.11 = f32[64,128]{1,0:T(8,128)} copy(f32[64,128]{1,0:T(8,128)} %get-tuple-element.5) | data formatting | bytes 65536
